TPU v7x, 32 devices: a whole 2x2x4 slice. The times are simulated.
32 devices in a mesh: grp: 4 (over z), dom: 8 (over y, x, core).
Axes of the slice: x: 2, y: 2, z: 4, core: 2. Of those that a mesh axis runs over, the one named last changes fastest.
Arguments:
- fluid_start: float32 [4, 256, 96, 128], P('grp', 'dom'), may hold values from -6 to 6
- fluid_rate: float32 [4, 256, 96, 128], P('grp', 'dom'), may hold values from 0.15 to 0.45
- fluid_coupling: float32 [4, 256, 128], P('grp', 'dom'), may hold values from 0.1 to 0.5
- solid_start: float32 [4, 128, 24, 128], P('grp', 'dom'), may hold values from -6 to 6
- solid_rate: float32 [4, 128, 24, 128], P('grp', 'dom'), may hold values from 0.2 to 0.6
- solid_coupling: float32 [4, 128, 128], P('grp', 'dom'), may hold values from 0.1 to 0.5
- solid_block: int32 [3072], P(('grp', 'dom')), may hold values from 0 to 127, as said below
- to_solid: bfloat16 [3072, 128, 128], P(('grp', 'dom')), as said below
- to_fluid: bfloat16 [3072, 128, 128], P(('grp', 'dom')), as said below
Outputs:
- fluid_temp: float32 [4, 256, 96, 128], P('grp', 'dom')
- solid_temp: float32 [4, 128, 24, 128], P('grp', 'dom')
Inputs may be any that keep to these rules, and one draw needn't show every extreme that they name: For segment s of fluid block x of its zone (x = (s // 3) mod 256), solid_block[s] lies within x // 2 - 2 to x // 2 + 2, taken modulo 128. `to_solid`: entry [s, i, j] is zero unless i and j differ by at most one; all entries are nonnegative. `to_fluid`: entry [s, i, j] is zero unless i and j differ by at most one; all entries are nonnegative.
All inputs are finite; a program needn't handle non-finite values.
Results may differ from a plain program's by a relative error of at most 0.0003.
Values may be sent and summed in bfloat16 or wider, within the bound.
A program may use at most 128 MiB of HBM per device.

v0:
```python
import functools

import jax
import jax.numpy as jnp
from jax import lax
from jax.experimental import pallas as pl
from jax.experimental.pallas import tpu as pltpu
from jax.sharding import PartitionSpec as P

PICARD = 4
CHUNKS = 4
MESH = pl.DeviceIdType.MESH
F32 = jnp.float32
BF16 = jnp.bfloat16


def body(
    n_grp, n_dom, per_block,
    fs, fr, fc, ss, sr, sc, off, ts, tf,
    fo, so,
    U0, U1, A, B, CPL, CF, Q,
    V0, V1, AS, BS, SCP, CFS, QS,
    MS, MF, WF, WS,
    PB, GB, LP0, LP1, LP2, LG, LGS, HF, HS,
    lsem, msem, s_init, r_init, s_row, r_row, s_face, r_face,
):
    g = lax.axis_index("grp")
    d = lax.axis_index("dom")
    R, Y = fs.shape[1], fs.shape[2]
    K, SY = ss.shape[1], ss.shape[2]
    dr = lax.rem(d + 1, n_dom)
    dl = lax.rem(d + n_dom - 1, n_dom)
    gu = lax.rem(g + 1, n_grp)
    gd = lax.rem(g + n_grp - 1, n_grp)
    has_r = d < n_dom - 1
    has_l = d > 0

    own = [
        (fs.at[0], U0.at[2 : R + 2, 8 : Y + 8]),
        (fr.at[0], B.at[2 : R + 2]),
        (fc.at[0], CPL.at[8 : R + 8]),
        (ss.at[0], V0.at[2 : K + 2, 8 : SY + 8]),
        (sr.at[0], BS.at[2 : K + 2]),
        (sc.at[0], SCP.at[8 : K + 8]),
    ]
    own = [pltpu.make_async_copy(a, b, lsem.at[i]) for i, (a, b) in enumerate(own)]
    for c in own:
        c.start()
    seg = ts.shape[0]
    part = seg // CHUNKS
    mats = []
    for q in range(CHUNKS):
        rows = pl.ds(q * part, part)
        mats.append(
            (
                pltpu.make_async_copy(tf.at[rows], MF.at[rows], msem.at[0, q]),
                pltpu.make_async_copy(ts.at[rows], MS.at[rows], msem.at[1, q]),
            )
        )
        for c in mats[-1]:
            c.start()

    for U, rows, wide in ((U0, R, Y), (U1, R, Y), (V0, K, SY), (V1, K, SY)):
        U[:, 0:8, :] = jnp.zeros((rows + 4, 8, 128), F32)
        U[:, wide + 8 : wide + 16, :] = jnp.zeros((rows + 4, 8, 128), F32)
    for U, rows, wide in ((U0, R, Y), (V0, K, SY)):
        U[0:2, 8 : wide + 8, :] = jnp.zeros((2, wide, 128), F32)
        U[rows + 2 : rows + 4, 8 : wide + 8, :] = jnp.zeros((2, wide, 128), F32)
    for U, rows, wide in ((B, R, Y), (BS, K, SY)):
        U[1, :, :] = jnp.zeros((wide, 128), F32)
        U[rows + 2, :, :] = jnp.zeros((wide, 128), F32)
    for C, rows in ((CPL, R), (SCP, K)):
        C[0:8, :] = jnp.zeros((8, 128), F32)
        C[rows + 8 : rows + 16, :] = jnp.zeros((8, 128), F32)
    CF[...] = jnp.zeros(CF.shape, F32)
    CFS[...] = jnp.zeros(CFS.shape, F32)
    WF[0] = jnp.zeros(WF.shape[1:], F32)
    WF[K + 1] = jnp.zeros(WF.shape[1:], F32)
    PB[...] = jnp.zeros(PB.shape, F32)

    barrier = pltpu.get_barrier_semaphore()
    around = [(g, dr), (g, dl)] + [(z, x) for z in (gu, gd) for x in (dl, d, dr)]
    for dev in around:
        pl.semaphore_signal(barrier, inc=1, device_id=dev, device_id_type=MESH)
    pl.semaphore_wait(barrier, len(around))

    def remote(src, dst, ssem, rsem, dev):
        return pltpu.make_async_remote_copy(
            src_ref=src, dst_ref=dst, send_sem=ssem, recv_sem=rsem,
            device_id=dev, device_id_type=MESH,
        )

    def init_list(side):
        if side == 0:
            dev, e, h = (g, dr), lambda n, w: pl.ds(n - w, w), lambda n, w, o: pl.ds(o - w, w)
        else:
            dev, e, h = (g, dl), lambda n, w: pl.ds(0, w), lambda n, w, o: pl.ds(n + o, w)
        pairs = [
            (fs.at[0, e(R, 2)], U0.at[h(R, 2, 2), 8 : Y + 8]),
            (fr.at[0, e(R, 1)], B.at[h(R, 1, 2)]),
            (fc.at[0, e(R, 8)], CPL.at[h(R, 8, 8)]),
            (ss.at[0, e(K, 2)], V0.at[h(K, 2, 2), 8 : SY + 8]),
            (sr.at[0, e(K, 1)], BS.at[h(K, 1, 2)]),
            (sc.at[0, e(K, 8)], SCP.at[h(K, 8, 8)]),
            (WF.at[K, 1], WF.at[0, 1]) if side == 0 else (WF.at[1, 0], WF.at[K + 1, 0]),
        ]
        return [
            remote(a, b, s_init.at[side, i], r_init.at[side, i], dev)
            for i, (a, b) in enumerate(pairs)
        ]

    inits = [init_list(0), init_list(1)]
    can_send = (has_r, has_l)
    can_recv = (has_l, has_r)

    for side in range(2):
        @pl.when(can_send[side])
        def _(side=side):
            for c in inits[side][:6]:
                c.start()

    lane = lax.broadcasted_iota(jnp.int32, (16, 128), 1)
    row16 = lax.broadcasted_iota(jnp.int32, (16, 128), 0)
    masks = [row16 == ((lane + t + 16) & 15) for t in (-1, 0, 1)]
    sub8 = lax.broadcasted_iota(jnp.int32, (8, 128), 0)

    def extract(c, _):
        for M, W, base in ((MF, WF, 1), (MS, WS, 0)):
            for p in range(2):
                acc = [jnp.zeros((8, 128), F32) for _ in range(3)]
                for k in range(per_block):
                    s = (2 * c + p) * per_block + k
                    folded = M[s, 0:16, :].astype(F32)
                    for r in range(1, 8):
                        folded = folded + M[s, 16 * r : 16 * r + 16, :].astype(F32)
                    at = sub8 == off[s]
                    for t in range(3):
                        line = jnp.sum(jnp.where(masks[t], folded, 0.0), axis=0, keepdims=True)
                        acc[t] = acc[t] + jnp.where(at, jnp.broadcast_to(line, (8, 128)), 0.0)
                for t in range(3):
                    W[c + base, p, t] = acc[t]
        return 0

    per = K // CHUNKS
    for q in range(CHUNKS):
        for c in mats[q]:
            c.wait()
        lax.fori_loop(q * per, (q + 1) * per, extract, 0)
    for side in range(2):
        @pl.when(can_send[side])
        def _(side=side):
            inits[side][6].start()
    for c in own:
        c.wait()

    def face_copies(i):
        sem = lambda j: (s_face.at[i, j], r_face.at[i, j])
        return [
            remote(GB.at[i], LG.at[i, 8 : K + 8], *sem(0), (gd, d)),
            remote(GB.at[i, K - 8 : K], LG.at[i, 0:8], *sem(1), (gd, dr)),
            remote(GB.at[i, 0:8], LG.at[i, K + 8 : K + 16], *sem(2), (gd, dl)),
            remote(PB.at[i], LP1.at[i], *sem(3), (gu, d)),
            remote(PB.at[i, K : K + 16], LP0.at[i], *sem(4), (gu, dr)),
            remote(PB.at[i, 0:16], LP2.at[i], *sem(5), (gu, dl)),
        ]

    def row_copies(i):
        sem = lambda s, j: (s_row.at[i - 1, s, j], r_row.at[i - 1, s, j])
        return [
            [
                remote(U0.at[R : R + 2, 8 : Y + 8], HF.at[i - 1, 0], *sem(0, 0), (g, dr)),
                remote(V0.at[K : K + 2, 8 : SY + 8], HS.at[i - 1, 0], *sem(0, 1), (g, dr)),
            ],
            [
                remote(U0.at[2:4, 8 : Y + 8], HF.at[i - 1, 1], *sem(1, 0), (g, dl)),
                remote(V0.at[2:4, 8 : SY + 8], HS.at[i - 1, 1], *sem(1, 1), (g, dl)),
            ],
        ]

    def build_solid_face(i):
        def step(c, _):
            line = V0[c + 2, SY + 7 : SY + 8, :]
            GB[i, pl.ds(c, 1), :] = line.astype(BF16).astype(F32)
            return 0
        lax.fori_loop(0, K, step, 0)

    def build_partial(i):
        def step(c, _):
            total = None
            for p in range(2):
                line = U0[2 * c + p + 2, 8:9, :].astype(BF16).astype(F32)
                wide = jnp.broadcast_to(line, (8, 128))
                views = (pltpu.roll(wide, 1, 1), wide, pltpu.roll(wide, 127, 1))
                for t in range(3):
                    term = views[t] * WS[c, p, t]
                    total = term if total is None else total + term
            PB[i, pl.ds(c + 6, 8), :] = PB[i, pl.ds(c + 6, 8), :] + total
            return 0
        lax.fori_loop(0, K, step, 0)

    def coefficients(U, X, Z, cpl, cf, wide, plane, first, last):
        at = lax.broadcasted_iota(jnp.int32, (wide, 128), 0) == plane
        def step(x, _):
            rate = Z[x]
            film = cpl[pl.ds(x + 6, 1), :]
            den = 1.0 + 6.0 * rate
            den = den + jnp.where(at, jnp.broadcast_to(film, (wide, 128)), 0.0)
            inv = 1.0 / den
            X[x] = U[x, 8 : wide + 8, :] * inv
            Z[x] = rate * inv
            cf[pl.ds(x + 6, 1), :] = film * inv[plane : plane + 1, :]
            return 0
        lax.fori_loop(first, last, step, 0)

    def sweep(src, dst, X, Z, wide, first, last):
        z = lax.broadcasted_iota(jnp.int32, (wide, 128), 1)
        at_l, at_r = z == 0, z == 127
        def step(x, _):
            c = src[x, 8 : wide + 8, :]
            s = src[x - 1, 8 : wide + 8, :] + src[x + 1, 8 : wide + 8, :]
            s = s + src[x, 7 : wide + 7, :] + src[x, 9 : wide + 9, :]
            s = s + jnp.where(at_l, 0.0, pltpu.roll(c, 1, 1))
            s = s + jnp.where(at_r, 0.0, pltpu.roll(c, 127, 1))
            dst[x, 8 : wide + 8, :] = X[x] + Z[x] * s
            return 0
        lax.fori_loop(first, last, step, 0)

    def patch(dst, q, row, first, last):
        def step(x, _):
            dst[x, row : row + 1, :] = dst[x, row : row + 1, :] + q[pl.ds(x + 6, 1), :]
            return 0
        lax.fori_loop(first, last, step, 0)

    coefficients(U0, A, B, CPL, CF, Y, 0, 2, R + 2)
    coefficients(V0, AS, BS, SCP, CFS, SY, SY - 1, 2, K + 2)

    for i in range(PICARD):
        build_solid_face(i)
        build_partial(i)
        faces = face_copies(i)
        for c in faces:
            c.start()
        rows = row_copies(i) if i else inits
        if i:
            for side in range(2):
                @pl.when(can_send[side])
                def _(side=side):
                    for c in rows[side]:
                        c.start()
        sweep(U0, U1, A, B, Y, 3, R + 1)
        sweep(V0, V1, AS, BS, SY, 3, K + 1)
        for side in range(2):
            @pl.when(can_recv[side])
            def _(side=side):
                for c in rows[side]:
                    c.wait_recv()
                if i:
                    at = 0 if side == 0 else R + 2
                    U0[at : at + 2, 8 : Y + 8, :] = HF[i - 1, side]
                    at = 0 if side == 0 else K + 2
                    V0[at : at + 2, 8 : SY + 8, :] = HS[i - 1, side]
        if i == 0:
            for at in (1, R + 2):
                coefficients(U0, A, B, CPL, CF, Y, 0, at, at + 1)
            for at in (1, K + 2):
                coefficients(V0, AS, BS, SCP, CFS, SY, SY - 1, at, at + 1)
        for first in (1, R + 1):
            sweep(U0, U1, A, B, Y, first, first + 2)
        for first in (1, K + 1):
            sweep(V0, V1, AS, BS, SY, first, first + 2)

        for c in faces[:3]:
            c.wait_recv()
        near = LG[i]
        LGS[0] = pltpu.roll(near, 1, 1)
        LGS[1] = near
        LGS[2] = pltpu.roll(near, 127, 1)

        def incoming(c, _):
            views = [LGS[t, pl.ds(c + 5, 8), :] for t in range(3)]
            for p in range(2):
                term = views[0] * WF[c, p, 0] + views[1] * WF[c, p, 1] + views[2] * WF[c, p, 2]
                line = jnp.sum(term, axis=0, keepdims=True)
                at = 2 * c + p + 6
                Q[pl.ds(at, 1), :] = CF[pl.ds(at, 1), :] * line
            return 0

        lax.fori_loop(0, K + 2, incoming, 0)
        patch(U1, Q, 8, 1, R + 3)
        for c in faces[3:]:
            c.wait_recv()
        QS[0:16, :] = CFS[0:16, :] * (LP1[i, 0:16, :] + LP0[i])
        QS[K : K + 16, :] = CFS[K : K + 16, :] * (LP1[i, K : K + 16, :] + LP2[i])
        patch(V1, QS, SY + 7, 1, K + 3)

        if i:
            for side in range(2):
                @pl.when(can_send[side])
                def _(side=side):
                    for c in rows[side]:
                        c.wait_send()
        sweep(U1, U0, A, B, Y, 2, R + 2)
        patch(U0, Q, 8, 2, R + 2)
        sweep(V1, V0, AS, BS, SY, 2, K + 2)
        patch(V0, QS, SY + 7, 2, K + 2)
        for c in faces:
            c.wait_send()

    for side in range(2):
        @pl.when(can_send[side])
        def _(side=side):
            for c in inits[side]:
                c.wait_send()
    outs = [
        pltpu.make_async_copy(U0.at[2 : R + 2, 8 : Y + 8], fo.at[0], lsem.at[0]),
        pltpu.make_async_copy(V0.at[2 : K + 2, 8 : SY + 8], so.at[0], lsem.at[1]),
    ]
    for c in outs:
        c.start()
    for c in outs:
        c.wait()


def local(n_grp, n_dom, fs, fr, fc, ss, sr, sc, blocks, ts, tf):
    R, Y = fs.shape[1], fs.shape[2]
    K, SY = ss.shape[1], ss.shape[2]
    seg = ts.shape[0]
    per_block = seg // R
    centre = K * lax.axis_index("dom") + jnp.arange(seg, dtype=jnp.int32) // (2 * per_block)
    off = (blocks - centre + 2) % (K * n_dom)
    v = lambda *s: pltpu.VMEM(s, F32)
    dma = lambda *s: pltpu.SemaphoreType.DMA(s)
    anyspec = pl.BlockSpec(memory_space=pl.ANY)
    return tuple(
        pl.pallas_call(
            functools.partial(body, n_grp, n_dom, per_block),
            out_shape=(
                jax.ShapeDtypeStruct(fs.shape, F32),
                jax.ShapeDtypeStruct(ss.shape, F32),
            ),
            in_specs=[anyspec] * 6 + [pl.BlockSpec(memory_space=pltpu.SMEM)] + [anyspec] * 2,
            out_specs=(anyspec, anyspec),
            scratch_shapes=[
                v(R + 4, Y + 16, 128), v(R + 4, Y + 16, 128), v(R + 4, Y, 128), v(R + 4, Y, 128),
                v(R + 16, 128), v(R + 16, 128), v(R + 16, 128),
                v(K + 4, SY + 16, 128), v(K + 4, SY + 16, 128), v(K + 4, SY, 128), v(K + 4, SY, 128),
                v(K + 16, 128), v(K + 16, 128), v(K + 16, 128),
                pltpu.VMEM(ts.shape, BF16), pltpu.VMEM(tf.shape, BF16),
                v(K + 2, 2, 3, 8, 128), v(K, 2, 3, 8, 128),
                v(PICARD, K + 16, 128), v(PICARD, K, 128),
                v(PICARD, 16, 128), v(PICARD, K + 16, 128), v(PICARD, 16, 128),
                v(PICARD, K + 16, 128), v(3, K + 16, 128),
                v(PICARD - 1, 2, 2, Y, 128), v(PICARD - 1, 2, 2, SY, 128),
                dma(6), dma(2, CHUNKS), dma(2, 7), dma(2, 7),
                dma(PICARD - 1, 2, 2), dma(PICARD - 1, 2, 2), dma(PICARD, 6), dma(PICARD, 6),
            ],
            compiler_params=pltpu.CompilerParams(collective_id=0, has_side_effects=True),
            name="cht",
        )(fs, fr, fc, ss, sr, sc, off, ts, tf)
    )


def solution(mesh):
    zone = P("grp", "dom", None, None)
    face = P("grp", "dom", None)
    flat = P(("grp", "dom"), None, None)
    return jax.shard_map(
        functools.partial(local, mesh.shape["grp"], mesh.shape["dom"]),
        mesh=mesh,
        in_specs=(zone, zone, face, zone, zone, face, P(("grp", "dom")), flat, flat),
        out_specs=(zone, zone),
        check_vma=False,
    )
```

profile of v0, /device:TPU:0, one launch (start us, length us, event | category | flops | bytes accessed | tf_op | source)
XLA Modules:
  0.0 63.4 jit_solution(4330487121805827826)
XLA Ops:
  0.6 1.2 %and_select_fusion.off = s32[96]{0:T(128)} fusion(s32[96]{0:T(128)} %param.15, s32[]{:T(128)S(6)} %mul_shard_map.3), kind=kLoop, calls=%fused_computation.2 | loop fusion | flops 2112 | bytes 772 | tf_op jit(solution)/shard_map/jit(remainder)/select_n | solution.py:330
  1.8 58.2 %cht.1 = (f32[1,32,96,128]{3,2,1,0:T(8,128)}, f32[1,16,24,128]{3,2,1,0:T(8,128)}) custom-call(f32[1,32,96,128]{3,2,1,0:T(8,128)} %fs.1, f32[1,32,96,128]{3,2,1,0:T(8,128)} %fr.1, f32[1,32,128]{2,1,0:T(8,128)} %fc.1, f32[1,16,24,128]{3,2,1,0:T(8,128)} %ss.1, f32[1,16,24,128]{3,2,1,0:T(8,128)} %sr.1, f32[1,16,128]{2,1,0:T(8,128)} %sc.1, ...), custom_call_target="tpu_custom_call" | custom-call | tf_op jit(solution)/shard_map/cht/pallas_call | solution.py:335
  60.0 0.0 copy-start
  60.0 2.7 %copy.13 = f32[1,32,96,128]{3,2,1,0:T(8,128)} copy(f32[1,32,96,128]{3,2,1,0:T(8,128)} %get-tuple-element.4) | data formatting | bytes 3145728
  62.7 0.0 copy-done
  62.7 0.7 %copy.14 = f32[1,16,24,128]{3,2,1,0:T(8,128)} copy(f32[1,16,24,128]{3,2,1,0:T(8,128)S(1)} %copy-done) | data formatting | bytes 393216
Async XLA Ops:
  60.0 2.7 %copy-start = (f32[1,16,24,128]{3,2,1,0:T(8,128)S(1)}, f32[1,16,24,128]{3,2,1,0:T(8,128)}, u32[]{:S(2)}) copy-start(f32[1,16,24,128]{3,2,1,0:T(8,128)} %get-tuple-element.5) | copy-start | bytes 589828
where the time goes:
time: 63.6 us; the launch traced here: 63.4 us
  Pallas kernels  58.2 us (92%)
  local copies, waits for them, and re-layouts  3.38 us (5%)
  other arithmetic  1.19 us (2%)
  between operations  0.65 us (1%)
    pallas_call x1, Pallas kernels, local(): pl.pallas_call(functools.partial(body, n_grp, n_dom, per_block), out_shap...  58.2 us
    unnamed x4, local copies, waits for them, and re-layouts  3.38 us

commit v1 on v0

--- a/solution.py
+++ b/solution.py
@@ -9,9 +9,24 @@
 
 PICARD = 4
 CHUNKS = 4
+UNROLL = 4
 MESH = pl.DeviceIdType.MESH
 F32 = jnp.float32
 BF16 = jnp.bfloat16
+
+
+def loop(first, last, unroll, step):
+    trips = (last - first) // unroll
+    def many(i, _):
+        for j in range(unroll):
+            step(first + i * unroll + j)
+        return 0
+    if trips > 1:
+        lax.fori_loop(0, trips, many, 0)
+    elif trips == 1:
+        many(0, 0)
+    for x in range(first + trips * unroll, last):
+        step(x)
 
 
 def body(
@@ -21,7 +36,7 @@
     U0, U1, A, B, CPL, CF, Q,
     V0, V1, AS, BS, SCP, CFS, QS,
     MS, MF, WF, WS,
-    PB, GB, LP0, LP1, LP2, LG, LGS, HF, HS,
+    PB, GB, FB, FS, LP0, LP1, LP2, LG, LGS, HF, HS,
     lsem, msem, s_init, r_init, s_row, r_row, s_face, r_face,
 ):
     g = lax.axis_index("grp")
@@ -130,10 +145,11 @@
                 acc = [jnp.zeros((8, 128), F32) for _ in range(3)]
                 for k in range(per_block):
                     s = (2 * c + p) * per_block + k
-                    folded = M[s, 0:16, :].astype(F32)
+                    folded = M[s, 0:16, :]
                     for r in range(1, 8):
-                        folded = folded + M[s, 16 * r : 16 * r + 16, :].astype(F32)
-                    at = sub8 == off[s]
+                        folded = folded + M[s, 16 * r : 16 * r + 16, :]
+                    folded = folded.astype(F32)
+                    at = sub8 == lax.rem(off[s] - (K * d + c) + 2 + K * n_dom, K * n_dom)
                     for t in range(3):
                         line = jnp.sum(jnp.where(masks[t], folded, 0.0), axis=0, keepdims=True)
                         acc[t] = acc[t] + jnp.where(at, jnp.broadcast_to(line, (8, 128)), 0.0)
@@ -178,29 +194,31 @@
         ]
 
     def build_solid_face(i):
-        def step(c, _):
+        for c in range(K):
             line = V0[c + 2, SY + 7 : SY + 8, :]
-            GB[i, pl.ds(c, 1), :] = line.astype(BF16).astype(F32)
-            return 0
-        lax.fori_loop(0, K, step, 0)
+            GB[i, c : c + 1, :] = line.astype(BF16).astype(F32)
 
     def build_partial(i):
-        def step(c, _):
+        for c in range(K):
+            for p in range(2):
+                FB[p, c : c + 1, :] = U0[2 * c + p + 2, 8:9, :]
+        for p in range(2):
+            line = FB[p].astype(BF16).astype(F32)
+            FS[0, p] = pltpu.roll(line, 1, 1)
+            FS[1, p] = line
+            FS[2, p] = pltpu.roll(line, 127, 1)
+        for c in range(K):
             total = None
             for p in range(2):
-                line = U0[2 * c + p + 2, 8:9, :].astype(BF16).astype(F32)
-                wide = jnp.broadcast_to(line, (8, 128))
-                views = (pltpu.roll(wide, 1, 1), wide, pltpu.roll(wide, 127, 1))
                 for t in range(3):
-                    term = views[t] * WS[c, p, t]
+                    wide = jnp.broadcast_to(FS[t, p, c : c + 1, :], (8, 128))
+                    term = wide * WS[c, p, t]
                     total = term if total is None else total + term
-            PB[i, pl.ds(c + 6, 8), :] = PB[i, pl.ds(c + 6, 8), :] + total
-            return 0
-        lax.fori_loop(0, K, step, 0)
+            PB[i, c + 6 : c + 14, :] = PB[i, c + 6 : c + 14, :] + total
 
     def coefficients(U, X, Z, cpl, cf, wide, plane, first, last):
         at = lax.broadcasted_iota(jnp.int32, (wide, 128), 0) == plane
-        def step(x, _):
+        def step(x):
             rate = Z[x]
             film = cpl[pl.ds(x + 6, 1), :]
             den = 1.0 + 6.0 * rate
@@ -209,27 +227,38 @@
             X[x] = U[x, 8 : wide + 8, :] * inv
             Z[x] = rate * inv
             cf[pl.ds(x + 6, 1), :] = film * inv[plane : plane + 1, :]
-            return 0
-        lax.fori_loop(first, last, step, 0)
-
-    def sweep(src, dst, X, Z, wide, first, last):
+        loop(first, last, 2, step)
+
+    def sweep(src, dst, X, Z, wide, first, last, q=None, plane=0):
         z = lax.broadcasted_iota(jnp.int32, (wide, 128), 1)
         at_l, at_r = z == 0, z == 127
-        def step(x, _):
+        tile = plane // 8 * 8
+        at = lax.broadcasted_iota(jnp.int32, (8, 128), 0) == plane - tile
+        def step(x):
             c = src[x, 8 : wide + 8, :]
             s = src[x - 1, 8 : wide + 8, :] + src[x + 1, 8 : wide + 8, :]
             s = s + src[x, 7 : wide + 7, :] + src[x, 9 : wide + 9, :]
             s = s + jnp.where(at_l, 0.0, pltpu.roll(c, 1, 1))
             s = s + jnp.where(at_r, 0.0, pltpu.roll(c, 127, 1))
-            dst[x, 8 : wide + 8, :] = X[x] + Z[x] * s
-            return 0
-        lax.fori_loop(first, last, step, 0)
+            out = X[x] + Z[x] * s
+            if q is None:
+                dst[x, 8 : wide + 8, :] = out
+            else:
+                line = jnp.broadcast_to(q[pl.ds(x + 6, 1), :], (8, 128))
+                piece = out[tile : tile + 8] + jnp.where(at, line, 0.0)
+                if tile:
+                    dst[x, 8 : tile + 8, :] = out[:tile]
+                dst[x, tile + 8 : tile + 16, :] = piece
+                if tile + 8 < wide:
+                    dst[x, tile + 16 : wide + 8, :] = out[tile + 8 :]
+        loop(first, last, UNROLL, step)
 
     def patch(dst, q, row, first, last):
-        def step(x, _):
-            dst[x, row : row + 1, :] = dst[x, row : row + 1, :] + q[pl.ds(x + 6, 1), :]
-            return 0
-        lax.fori_loop(first, last, step, 0)
+        for low in range(first, last, 8):
+            some = range(low, min(low + 8, last))
+            new = [dst[x, row : row + 1, :] + q[x + 6 : x + 7, :] for x in some]
+            for x, line in zip(some, new):
+                dst[x, row : row + 1, :] = line
 
     coefficients(U0, A, B, CPL, CF, Y, 0, 2, R + 2)
     coefficients(V0, AS, BS, SCP, CFS, SY, SY - 1, 2, K + 2)
@@ -241,12 +270,6 @@
         for c in faces:
             c.start()
         rows = row_copies(i) if i else inits
-        if i:
-            for side in range(2):
-                @pl.when(can_send[side])
-                def _(side=side):
-                    for c in rows[side]:
-                        c.start()
         sweep(U0, U1, A, B, Y, 3, R + 1)
         sweep(V0, V1, AS, BS, SY, 3, K + 1)
         for side in range(2):
@@ -276,16 +299,15 @@
         LGS[1] = near
         LGS[2] = pltpu.roll(near, 127, 1)
 
-        def incoming(c, _):
+        def incoming(c):
             views = [LGS[t, pl.ds(c + 5, 8), :] for t in range(3)]
             for p in range(2):
                 term = views[0] * WF[c, p, 0] + views[1] * WF[c, p, 1] + views[2] * WF[c, p, 2]
                 line = jnp.sum(term, axis=0, keepdims=True)
                 at = 2 * c + p + 6
                 Q[pl.ds(at, 1), :] = CF[pl.ds(at, 1), :] * line
-            return 0
-
-        lax.fori_loop(0, K + 2, incoming, 0)
+
+        loop(0, K + 2, 6, incoming)
         patch(U1, Q, 8, 1, R + 3)
         for c in faces[3:]:
             c.wait_recv()
@@ -299,10 +321,17 @@
                 def _(side=side):
                     for c in rows[side]:
                         c.wait_send()
-        sweep(U1, U0, A, B, Y, 2, R + 2)
-        patch(U0, Q, 8, 2, R + 2)
-        sweep(V1, V0, AS, BS, SY, 2, K + 2)
-        patch(V0, QS, SY + 7, 2, K + 2)
+        for first in (2, R):
+            sweep(U1, U0, A, B, Y, first, first + 2, Q, 0)
+        sweep(V1, V0, AS, BS, SY, 2, K + 2, QS, SY - 1)
+        if i + 1 < PICARD:
+            ahead = row_copies(i + 1)
+            for side in range(2):
+                @pl.when(can_send[side])
+                def _(side=side):
+                    for c in ahead[side]:
+                        c.start()
+        sweep(U1, U0, A, B, Y, 4, R, Q, 0)
         for c in faces:
             c.wait_send()
 
@@ -326,8 +355,6 @@
     K, SY = ss.shape[1], ss.shape[2]
     seg = ts.shape[0]
     per_block = seg // R
-    centre = K * lax.axis_index("dom") + jnp.arange(seg, dtype=jnp.int32) // (2 * per_block)
-    off = (blocks - centre + 2) % (K * n_dom)
     v = lambda *s: pltpu.VMEM(s, F32)
     dma = lambda *s: pltpu.SemaphoreType.DMA(s)
     anyspec = pl.BlockSpec(memory_space=pl.ANY)
@@ -348,6 +375,7 @@
                 pltpu.VMEM(ts.shape, BF16), pltpu.VMEM(tf.shape, BF16),
                 v(K + 2, 2, 3, 8, 128), v(K, 2, 3, 8, 128),
                 v(PICARD, K + 16, 128), v(PICARD, K, 128),
+                v(2, K, 128), v(3, 2, K, 128),
                 v(PICARD, 16, 128), v(PICARD, K + 16, 128), v(PICARD, 16, 128),
                 v(PICARD, K + 16, 128), v(3, K + 16, 128),
                 v(PICARD - 1, 2, 2, Y, 128), v(PICARD - 1, 2, 2, SY, 128),
@@ -356,7 +384,7 @@
             ],
             compiler_params=pltpu.CompilerParams(collective_id=0, has_side_effects=True),
             name="cht",
-        )(fs, fr, fc, ss, sr, sc, off, ts, tf)
+        )(fs, fr, fc, ss, sr, sc, blocks, ts, tf)
     )
 
 

time: 63.6 us -> 41.5 us (0.65)
  Pallas kernels: 58.2 us -> 37.3 us
  other arithmetic: 1.19 us -> 0 us
    pallas_call x1, Pallas kernels: 58.2 us -> 37.3 us  [local(): pl.pallas_call(functools.partial(body, n_grp, n_dom, per_block), out_shap...]
    select_n x1 -> x0, other arithmetic: 1.19 us -> none  [local(): off = (blocks - centre + 2) % (K * n_dom)]
where the time goes in v1:
time: 41.5 us; the launch traced here: 41.3 us
  Pallas kernels  37.3 us (90%)
  local copies, waits for them, and re-layouts  3.38 us (8%)
  between operations  0.65 us (2%)
    pallas_call x1, Pallas kernels, local(): pl.pallas_call(functools.partial(body, n_grp, n_dom, per_block), out_shap...  37.3 us
    unnamed x4, local copies, waits for them, and re-layouts  3.38 us

profile of v1, /device:TPU:0, one launch (start us, length us, event | category | flops | bytes accessed | tf_op | source)
XLA Modules:
  0.0 41.3 jit_solution(17713258404026105831)
XLA Ops:
  0.6 37.3 %cht.1 = (f32[1,32,96,128]{3,2,1,0:T(8,128)}, f32[1,16,24,128]{3,2,1,0:T(8,128)}) custom-call(f32[1,32,96,128]{3,2,1,0:T(8,128)} %fs.1, f32[1,32,96,128]{3,2,1,0:T(8,128)} %fr.1, f32[1,32,128]{2,1,0:T(8,128)} %fc.1, f32[1,16,24,128]{3,2,1,0:T(8,128)} %ss.1, f32[1,16,24,128]{3,2,1,0:T(8,128)} %sr.1, f32[1,16,128]{2,1,0:T(8,128)} %sc.1, s32[96]{0:T(128)} %off.1, ...), custom_call_target="tpu_custom_call" | custom-call | tf_op jit(solution)/shard_map/cht/pallas_call | solution.py:362
  38.0 0.0 copy-start
  38.0 2.7 %copy.13 = f32[1,32,96,128]{3,2,1,0:T(8,128)} copy(f32[1,32,96,128]{3,2,1,0:T(8,128)} %get-tuple-element.4) | data formatting | bytes 3145728
  40.7 0.0 copy-done
  40.7 0.7 %copy.14 = f32[1,16,24,128]{3,2,1,0:T(8,128)} copy(f32[1,16,24,128]{3,2,1,0:T(8,128)S(1)} %copy-done) | data formatting | bytes 393216
Async XLA Ops:
  38.0 2.7 %copy-start = (f32[1,16,24,128]{3,2,1,0:T(8,128)S(1)}, f32[1,16,24,128]{3,2,1,0:T(8,128)}, u32[]{:S(2)}) copy-start(f32[1,16,24,128]{3,2,1,0:T(8,128)} %get-tuple-element.5) | copy-start | bytes 589828
